TPU v7x, 32 devices: a whole 2x2x4 slice. The times are simulated.
32 devices in a mesh: slab: 8 (over y, x, core), lev: 4 (over z).
Axes of the slice: x: 2, y: 2, z: 4, core: 2. Of those that a mesh axis runs over, the one named last changes fastest.
Arguments:
- ensemble: float32 [80, 16, 18432], P(None, 'lev', 'slab'), may hold values from -6 to 6
- obs_cell: int32 [2, 256], replicated, may hold values from 0 to 294911, as said below
- obs_value: float32 [2, 256], replicated, may hold values from -6 to 6
- obs_var: float32 [2, 256], replicated, may hold values from 0.3 to 3
- obs_frac: float32 [2, 256], replicated, may hold values from 0 to 1
- loc_column: bfloat16 [2, 256, 18432], P(None, 'lev', 'slab'), may hold values from 0 to 1
- loc_level: float32 [2, 256, 16], P(None, None, 'lev'), may hold values from 0.2 to 1
Outputs:
- analysis: float32 [80, 16, 18432], P(None, 'lev', 'slab')
- prior_mean: float32 [2, 256], replicated
Inputs may be any that keep to these rules, and one draw needn't show every extreme that they name: `obs_cell`: in each block, every device's cells (a level band of 4 levels and a slab of 2304 columns) hold at least one observation, and one of them lies in the slab's last column.
All inputs are finite; a program needn't handle non-finite values.
Results may differ from a plain program's by a relative error of at most 0.0055.
Values may be sent and summed in bfloat16 or wider, within the bound.
A program may use at most 64 MiB of HBM per device.

v0:
```python
import functools

import jax
import jax.numpy as jnp
from jax import lax
from jax.experimental import pallas as pl
from jax.experimental.pallas import tpu as pltpu
from jax.sharding import PartitionSpec as P

MESH = pl.DeviceIdType.MESH
LANES = 128
F32 = jnp.float32
BF16 = jnp.bfloat16


def pick_kernel(block, members, lev_rows, n_slab, cell_ref, frac_ref, ens_ref, out_ref, acc, list_ref):
    n_obs = cell_ref.shape[1]
    raw = len(ens_ref.shape) == 3
    tiles = ens_ref.shape[2] // LANES if raw else ens_ref.shape[0] // (members * lev_rows)
    slab_cols = tiles * LANES
    total = slab_cols * n_slab
    base = lax.axis_index("lev") * (lev_rows * total)
    col_base = lax.axis_index("slab") * slab_cols
    acc[...] = jnp.zeros_like(acc)
    lane_ids = lax.broadcasted_iota(jnp.int32, (members, LANES), 1)

    def place(j):
        rest = cell_ref[block, j] - base
        row = jnp.int32(0)
        for level in range(1, lev_rows):
            row = row + (rest >= level * total).astype(jnp.int32)
        col = rest - row * total
        following = jnp.where(col + 1 == total, 0, col + 1)
        first, second = col - col_base, following - col_base
        in_band = (rest >= 0) & (rest < lev_rows * total)
        has_first = in_band & (first >= 0) & (first < slab_cols)
        has_second = in_band & (second >= 0) & (second < slab_cols)
        return row, first, second, has_first, has_second

    def scan(j, count):
        _, _, _, has_first, has_second = place(j)
        list_ref[count] = j
        return count + (has_first | has_second).astype(jnp.int32)

    count = lax.fori_loop(0, n_obs, scan, jnp.int32(0), unroll=8)

    def body(at, carry):
        j = list_ref[at]
        row, first, second, has_first, has_second = place(j)
        frac = frac_ref[block, j]
        tile_at = lax.shift_right_logical(j, 7)
        lane_at = j & (LANES - 1)

        def share(local, weight, mine, level):
            local = jnp.where(mine, local, 0)
            tile = lax.shift_right_logical(local, 7)
            if raw:
                window = ens_ref[:, level, pl.ds(pl.multiple_of(tile * LANES, LANES), LANES)]
            else:
                window = ens_ref[pl.ds(tile * lev_rows + row, members, stride=tiles * lev_rows), :]
            moved = pltpu.roll(window, (lane_at - (local & (LANES - 1))) & (LANES - 1), 1)
            return moved * jnp.where(mine, weight, 0.0)

        def put(level):
            value = share(first, 1.0 - frac, has_first, level) + share(second, frac, has_second, level)
            old = acc[tile_at, :members, :]
            acc[tile_at, :members, :] = jnp.where(lane_ids == lane_at, value, old)

        if raw:
            for level in range(lev_rows):
                pl.when(row == level)(functools.partial(put, level))
        else:
            put(0)
        return carry

    lax.fori_loop(0, count, body, 0)
    for t in range(n_obs // LANES):
        out_ref[t * LANES : (t + 1) * LANES, :] = acc[t].T


def pick(block, n_slab, members, lev_rows, cells, fracs, flat):
    n_obs = cells.shape[1]
    return pl.pallas_call(
        functools.partial(pick_kernel, block, members, lev_rows, n_slab),
        out_shape=jax.ShapeDtypeStruct((n_obs, LANES), F32),
        in_specs=[
            pl.BlockSpec(memory_space=pltpu.SMEM),
            pl.BlockSpec(memory_space=pltpu.SMEM),
            pl.BlockSpec(memory_space=pltpu.VMEM),
        ],
        out_specs=pl.BlockSpec(memory_space=pltpu.VMEM),
        scratch_shapes=[pltpu.VMEM((n_obs // LANES, LANES, LANES), F32), pltpu.SMEM((n_obs + 1,), jnp.int32)],
        name="pick",
    )(cells, fracs, flat)


def exchange_kernel(
    n_slab, n_lev, pieces, part_ref, loc_ref, prior_ref, gat_ref, landed, own,
    scat_send, scat_recv, cast_send, cast_recv, up_send, down_send, line_recv,
):
    n = n_slab * n_lev
    slab, lev = lax.axis_index("slab"), lax.axis_index("lev")
    me = slab * n_lev + lev
    rows = loc_ref.shape[1]
    cut = rows // pieces

    def peer(k):
        p = lax.rem(me + k, n)
        return p, (p // n_lev, lax.rem(p, n_lev))

    barrier = pltpu.get_barrier_semaphore()

    def greet(k, c):
        _, where = peer(k)
        pl.semaphore_signal(barrier, inc=1, device_id=where, device_id_type=MESH)
        return c

    lax.fori_loop(1, n, greet, 0)
    pl.semaphore_wait(barrier, n - 1)

    def scatter(k):
        p, where = peer(k)
        return pltpu.make_async_remote_copy(
            src_ref=part_ref.at[p], dst_ref=landed.at[k], send_sem=scat_send.at[k],
            recv_sem=scat_recv.at[k], device_id=where, device_id_type=MESH)

    def cast(k):
        _, where = peer(k)
        return pltpu.make_async_remote_copy(
            src_ref=own, dst_ref=prior_ref.at[me], send_sem=cast_send.at[k],
            recv_sem=cast_recv.at[k], device_id=where, device_id_type=MESH)

    def each(act):
        def body(k, c):
            act(k)
            return c
        lax.fori_loop(1, n, body, 0)

    def slot(source, h):
        return gat_ref.at[pl.ds(pl.multiple_of(source * rows + h * cut, cut), cut), :]

    def hop(source, h, first, step):
        src = loc_ref.at[0, pl.ds(h * cut, cut), :] if first else slot(source, h)
        sems = up_send if step > 0 else down_send
        return pltpu.make_async_remote_copy(
            src_ref=src, dst_ref=slot(source, h), send_sem=sems.at[source, h],
            recv_sem=line_recv.at[source, h], device_id=(slab, lev + step), device_id_type=MESH)

    each(lambda k: scatter(k).start())
    for h in range(pieces):
        @pl.when(lev < n_lev - 1)
        def _():
            hop(lev, h, True, 1).start()

        @pl.when(lev > 0)
        def _():
            hop(lev, h, True, -1).start()

    gat_ref[pl.ds(pl.multiple_of(lev * rows, rows), rows), :] = loc_ref[0]

    each(lambda k: scatter(k).wait_recv())
    landed[0] = part_ref[me]
    own[...] = jnp.sum(landed[...], axis=0)
    each(lambda k: cast(k).start())
    prior_ref[me] = own[...]

    for s in range(1, n_lev):
        for h in range(pieces):
            @pl.when(lev - s >= 0)
            def _():
                hop(lev - s, h, False, 1).wait_recv()

                @pl.when(lev < n_lev - 1)
                def _():
                    hop(lev - s, h, False, 1).start()

            @pl.when(lev + s <= n_lev - 1)
            def _():
                hop(lev + s, h, False, -1).wait_recv()

                @pl.when(lev > 0)
                def _():
                    hop(lev + s, h, False, -1).start()

    each(lambda k: cast(k).wait_recv())
    each(lambda k: scatter(k).wait_send())
    each(lambda k: cast(k).wait_send())
    for s in range(n_lev):
        for h in range(pieces):
            @pl.when((lev - s >= 0) & (lev < n_lev - 1))
            def _():
                hop(lev - s, h, s == 0, 1).wait_send()

            @pl.when((lev + s <= n_lev - 1) & (lev > 0))
            def _():
                hop(lev + s, h, s == 0, -1).wait_send()


def exchange(block, n_slab, n_lev, part, loc):
    n = n_slab * n_lev
    n_obs = part.shape[0]
    per = n_obs // n
    rows, cols = loc.shape[1:]
    pieces = 2
    prior, gathered = pl.pallas_call(
        functools.partial(exchange_kernel, n_slab, n_lev, pieces),
        grid=(1,),
        out_shape=[
            jax.ShapeDtypeStruct((n, per, LANES), F32),
            jax.ShapeDtypeStruct((n_obs, cols), BF16),
        ],
        in_specs=[
            pl.BlockSpec((n, per, LANES), lambda i: (0, 0, 0)),
            pl.BlockSpec((1, rows, cols), lambda i: (block, 0, 0)),
        ],
        out_specs=[
            pl.BlockSpec((n, per, LANES), lambda i: (0, 0, 0)),
            pl.BlockSpec((n_obs, cols), lambda i: (0, 0)),
        ],
        scratch_shapes=[
            pltpu.VMEM((n, per, LANES), F32),
            pltpu.VMEM((per, LANES), F32),
            pltpu.SemaphoreType.DMA((n,)),
            pltpu.SemaphoreType.DMA((n,)),
            pltpu.SemaphoreType.DMA((n,)),
            pltpu.SemaphoreType.DMA((n,)),
            pltpu.SemaphoreType.DMA((n_lev, pieces)),
            pltpu.SemaphoreType.DMA((n_lev, pieces)),
            pltpu.SemaphoreType.DMA((n_lev, pieces)),
        ],
        compiler_params=pltpu.CompilerParams(collective_id=block, has_side_effects=True),
        name="exchange",
    )(part.reshape(n, per, LANES), loc)
    return prior.reshape(n_obs, LANES), gathered


def update_kernel(block, lev_rows, raw_in, raw_out, prior_ref, value_ref, var_ref, lev_ref, old_ref, loc_ref, ens_ref, out_ref, mean_ref, dev_s, gain_s, lev_s):
    members = ens_ref.shape[0]
    n_obs = prior_ref.shape[0]
    tiles = loc_ref.shape[1] // LANES
    group = tiles * lev_rows

    @pl.when(pl.program_id(0) == 0)
    def _():
        def column(ref):
            return jnp.broadcast_to(ref[block : block + 1, :], (8, n_obs)).T[:, :1]

        value, var = column(value_ref), column(var_ref)
        prior = prior_ref[...]
        live = lax.broadcasted_iota(jnp.int32, prior.shape, 1) < members
        mean = jnp.sum(jnp.where(live, prior, 0.0), axis=1, keepdims=True) / members
        deviation = jnp.where(live, prior - mean, 0.0)
        spread = jnp.sum(deviation * deviation, axis=1, keepdims=True) / (members - 1.0)
        total = spread + var
        shrink = 1.0 / (1.0 + jnp.sqrt(var / total))
        gain = ((value - mean) - deviation * shrink) / (total * (members - 1.0))
        dev_s[...] = deviation.astype(BF16)
        gain_s[...] = gain.T.astype(BF16)
        mean_ref[...] = old_ref[...]
        mean_ref[block : block + 1, :] = jnp.broadcast_to(mean, (n_obs, LANES)).T[:1, :]
        for level in range(lev_rows):
            lev_s[level] = jnp.broadcast_to(lev_ref[level : level + 1, :], (LANES, n_obs)).T

    dev = dev_s[:, :members]
    gain = gain_s[:members, :]
    rows_in = None if raw_in else ens_ref.reshape(members * group, LANES)
    rows_out = None if raw_out else out_ref.reshape(members * group, LANES)
    loc = loc_ref[...].astype(F32)
    for level in range(lev_rows):
        spots = [pl.ds(t * lev_rows + level, members, stride=group) for t in range(tiles)]
        if raw_in:
            now = ens_ref[:, level, :]
        else:
            now = jnp.concatenate([rows_in[spot, :] for spot in spots], axis=1)
        centred = (now - jnp.sum(now, axis=0, keepdims=True) / members).astype(BF16)
        cross = jnp.dot(dev, centred, preferred_element_type=F32)
        height = jnp.concatenate([lev_s[level]] * tiles, axis=1)
        mixed = ((height * loc) * cross).astype(BF16)
        new = now + jnp.dot(gain, mixed, preferred_element_type=F32)
        if raw_out:
            out_ref[:, level, :] = new
        else:
            for t, spot in enumerate(spots):
                rows_out[spot, :] = new[:, t * LANES : (t + 1) * LANES]


def update(block, n_blocks, lev_rows, prior, values, variances, levels, olds, gathered, state):
    members = state.shape[0]
    n_obs = prior.shape[0]
    tiles = next(t for t in (6, 4, 2) if gathered.shape[1] % (t * LANES) == 0)
    group = tiles * lev_rows
    cols = gathered.shape[1]
    steps = cols // (tiles * LANES)
    raw_in, raw_out = block == 0, block == n_blocks - 1
    raw_spec = pl.BlockSpec((members, lev_rows, tiles * LANES), lambda i: (0, 0, i))
    row_spec = pl.BlockSpec((members, group, LANES), lambda i: (0, i, 0))
    out_dims = (members, lev_rows, cols) if raw_out else (members, steps * group, LANES)
    return pl.pallas_call(
        functools.partial(update_kernel, block, lev_rows, raw_in, raw_out),
        grid=(steps,),
        out_shape=[
            jax.ShapeDtypeStruct(out_dims, F32),
            jax.ShapeDtypeStruct(values.shape, F32),
        ],
        in_specs=[
            pl.BlockSpec((n_obs, LANES), lambda i: (0, 0)),
            pl.BlockSpec(values.shape, lambda i: (0, 0)),
            pl.BlockSpec(values.shape, lambda i: (0, 0)),
            pl.BlockSpec((None, lev_rows, n_obs), lambda i: (block, 0, 0)),
            pl.BlockSpec(olds.shape, lambda i: (0, 0)),
            pl.BlockSpec((n_obs, tiles * LANES), lambda i: (0, i)),
            raw_spec if raw_in else row_spec,
        ],
        out_specs=[
            raw_spec if raw_out else row_spec,
            pl.BlockSpec(values.shape, lambda i: (0, 0)),
        ],
        scratch_shapes=[pltpu.VMEM((n_obs, LANES), BF16), pltpu.VMEM((LANES, n_obs), BF16), pltpu.VMEM((lev_rows, n_obs, LANES), F32)],
        compiler_params=pltpu.CompilerParams(dimension_semantics=("arbitrary",)),
        name="update",
    )(prior, values, variances, levels, olds, gathered, state)


def solution(mesh):
    n_slab, n_lev = mesh.shape["slab"], mesh.shape["lev"]

    def on_device(ensemble, obs_cell, obs_value, obs_var, obs_frac, loc_column, loc_level):
        members, lev_rows, cols = ensemble.shape
        n_blocks = obs_cell.shape[0]
        state = ensemble
        means, heights = obs_value, loc_level.transpose(0, 2, 1)
        for block in range(n_blocks):
            flat = state if block == 0 else state.reshape(members * cols // LANES * lev_rows, LANES)
            part = pick(block, n_slab, members, lev_rows, obs_cell, obs_frac, flat)
            prior, gathered = exchange(block, n_slab, n_lev, part, loc_column)
            state, means = update(block, n_blocks, lev_rows, prior, obs_value, obs_var, heights, means, gathered, state)
        return state, means

    in_specs = (
        P(None, "lev", "slab"), P(), P(), P(), P(),
        P(None, "lev", "slab"), P(None, None, "lev"),
    )
    return jax.shard_map(
        on_device, mesh=mesh, in_specs=in_specs,
        out_specs=(P(None, "lev", "slab"), P()), check_vma=False,
    )
```

profile of v0, /device:TPU:0, one launch (start us, length us, event | category | flops | bytes accessed | tf_op | source)
XLA Modules:
  0.0 101.2 jit_solution(15538248033473496140)
XLA Ops:
  0.6 10.6 %pick.2 = f32[256,128]{1,0:T(8,128)} custom-call(s32[2,256]{1,0:T(2,128)} %cell_ref.3, f32[2,256]{1,0:T(2,128)} %frac_ref.3, f32[80,4,2304]{2,1,0:T(4,128)} %ens_ref.3), custom_call_target="tpu_custom_call" | custom-call | tf_op jit(solution)/shard_map/pick/pallas_call | solution.py:83
  11.2 34.5 %exchange.2 = (f32[32,8,128]{2,1,0:T(8,128)}, bf16[256,2304]{1,0:T(8,128)(2,1)}) custom-call(f32[32,8,128]{2,1,0:T(8,128)} %bitcast.7, bf16[2,64,2304]{2,1,0:T(8,128)(2,1)} %loc_ref.3), custom_call_target="tpu_custom_call" | custom-call | tf_op jit(solution)/shard_map/exchange/pallas_call | solution.py:205
  45.7 8.0 %update.2 = (f32[80,72,128]{2,1,0:T(8,128)}, f32[2,256]{1,0:T(2,128)}) custom-call(f32[256,128]{1,0:T(8,128)} %bitcast.10, f32[2,256]{1,0:T(2,128)} %value_ref.3, f32[2,256]{1,0:T(2,128)} %var_ref.3, f32[2,4,256]{2,1,0:T(4,128)} %bitcast.11, f32[2,256]{1,0:T(2,128)} %value_ref.3, bf16[256,2304]{1,0:T(8,128)(2,1)} %get-tuple-element.9.loc_ref, ...), custom_call_target="tpu_custom_call" | custom-call | tf_op jit(solution)/shard_map/update/pallas_call | solution.py:298
  53.7 9.1 %pick.3 = f32[256,128]{1,0:T(8,128)} custom-call(s32[2,256]{1,0:T(2,128)} %cell_ref.3, f32[2,256]{1,0:T(2,128)} %frac_ref.3, f32[5760,128]{1,0:T(8,128)} %bitcast.6), custom_call_target="tpu_custom_call" | custom-call | tf_op jit(solution)/shard_map/pick/pallas_call | solution.py:83
  62.8 31.0 %exchange.3 = (f32[32,8,128]{2,1,0:T(8,128)}, bf16[256,2304]{1,0:T(8,128)(2,1)}) custom-call(f32[32,8,128]{2,1,0:T(8,128)} %bitcast.8, bf16[2,64,2304]{2,1,0:T(8,128)(2,1)} %loc_ref.3), custom_call_target="tpu_custom_call" | custom-call | tf_op jit(solution)/shard_map/exchange/pallas_call | solution.py:205
  93.8 7.4 %update.3 = (f32[80,4,2304]{2,1,0:T(4,128)}, f32[2,256]{1,0:T(2,128)}) custom-call(f32[256,128]{1,0:T(8,128)} %bitcast.9, f32[2,256]{1,0:T(2,128)} %value_ref.3, f32[2,256]{1,0:T(2,128)} %var_ref.3, f32[2,4,256]{2,1,0:T(4,128)} %bitcast.12, f32[2,256]{1,0:T(2,128)} %get-tuple-element.12.old_ref, bf16[256,2304]{1,0:T(8,128)(2,1)} %get-tuple-element.13.loc_ref, ...), custom_call_target="tpu_custom_call" | custom-call | tf_op jit(solution)/shard_map/update/pallas_call | solution.py:298
where the time goes:
time: 101 us
  Pallas kernels  101 us (100%)
    pallas_call x2, Pallas kernels, exchange(): pl.pallas_call(functools.partial(exchange_kernel, n_slab, n_lev, pieces),...  65.5 us
    pallas_call x2, Pallas kernels, pick(): pl.pallas_call(functools.partial(pick_kernel, block, members, lev_rows, n...  19.7 us
    pallas_call x2, Pallas kernels, update(): pl.pallas_call(functools.partial(update_kernel, block, lev_rows, raw_in,...  15.4 us

commit v1 on v0

v1 whole, which is shorter than its diff:
```python
import functools

import jax
import jax.numpy as jnp
from jax import lax
from jax.experimental import pallas as pl
from jax.experimental.pallas import tpu as pltpu
from jax.sharding import PartitionSpec as P

MESH = pl.DeviceIdType.MESH
LANES = 128
SUBLANES = 8
F32 = jnp.float32
BF16 = jnp.bfloat16
SKEW = 3
STEPS_FIRST = (1, 2, 1)
STEPS_LATER = (2, 3, 2)


def kernel(
    n_slab, n_lev, cell_ref, frac_ref, value_ref, var_ref, lev_ref, ens_hbm, loc_hbm, out_ref, mean_ref,
    raw, plain, gat, keys, acc, part, landed, zown, zland, own, prior, dev_s, gain_s, lev_s,
    load_sem, line_recv, first_send, line_send, scat_send, scat_recv, z_send, z_recv, cast_send, cast_recv, out_sem,
):
    members, lev_rows, cols = raw.shape
    n_blocks, n_obs = cell_ref.shape
    rows = loc_hbm.shape[1]
    tiles = cols // LANES
    chunks = line_recv.shape[2]
    width = cols // chunks
    wide = width // LANES
    total = cols * n_slab
    slots = n_obs // n_slab
    lag = SKEW * (n_lev - 2)
    steps = chunks + lag
    obs_tiles = n_obs // LANES
    slab, lev = lax.axis_index("slab"), lax.axis_index("lev")

    loads = [
        pltpu.make_async_copy(loc_hbm.at[b], gat.at[b, pl.ds(pl.multiple_of(lev * rows, rows), rows), :], load_sem.at[b])
        for b in range(n_blocks)
    ]
    loads.append(pltpu.make_async_copy(ens_hbm, raw, load_sem.at[n_blocks]))
    for load in loads:
        load.start()

    def on_slab(k):
        p = lax.rem(slab + k, n_slab)
        return p, (p, lev)

    def on_line(k):
        return (slab, lax.rem(lev + k, n_lev))

    barrier = pltpu.get_barrier_semaphore()
    for k in range(1, n_lev):
        pl.semaphore_signal(barrier, inc=1, device_id=on_line(k), device_id_type=MESH)
    for k in range(1, n_slab):
        pl.semaphore_signal(barrier, inc=1, device_id=on_slab(k)[1], device_id_type=MESH)
    pl.semaphore_wait(barrier, n_slab + n_lev - 2)

    def hop(step, b, source, c, sem):
        spot = gat.at[
            b, pl.ds(pl.multiple_of(source * rows, rows), rows), pl.ds(pl.multiple_of(c * width, width), width)
        ]
        return pltpu.make_async_remote_copy(
            src_ref=spot, dst_ref=spot, send_sem=sem, recv_sem=line_recv.at[b, source, c],
            device_id=(slab, lev + step), device_id_type=MESH)

    ends = ((0, 1, lev < n_lev - 1), (1, -1, lev > 0))

    def send_own_first(c, carry):
        for way, step, alive in ends:
            @pl.when(alive)
            def _():
                hop(step, 0, lev, c, first_send.at[way, c]).start()
        return carry

    loads[0].wait()
    lax.fori_loop(0, chunks, send_own_first, 0)

    def send(way, step, d, b, source, c, order):
        sem = line_send.at[way, d, lax.rem(order, 2)]

        @pl.when(order >= 2)
        def _():
            hop(step, b, source, c, sem).wait_send()

        hop(step, b, source, c, sem).start()

    def forward(b, s):
        if b + 1 < n_blocks:
            pass
        for d in range(1, n_lev):
            c = s - (d - 1) * SKEW

            @pl.when((c >= 0) & (c < chunks))
            def _():
                for way, step, alive in ends:
                    source = lev - step * d

                    @pl.when((source >= 0) & (source < n_lev))
                    def _():
                        hop(step, b, source, c, line_send.at[way, d, 0]).wait_recv()
                        if d < n_lev - 1:
                            @pl.when(alive)
                            def _():
                                send(way, step, d, b, source, c, c + b * chunks)

        for nxt in range(1, n_blocks):
            c = s + (b - nxt + 1) * steps - chunks

            @pl.when((c >= 0) & (c < chunks))
            def _():
                for way, step, alive in ends:
                    @pl.when(alive)
                    def _():
                        send(way, step, 0, nxt, lev, c, c + (nxt - 1) * chunks)

    def forwards(b, start, stop):
        def body(s, carry):
            forward(b, s)
            return carry
        lax.fori_loop(start, stop, body, 0)

    def locate(b):
        cell = jnp.broadcast_to(cell_ref[b : b + 1, :], (SUBLANES, n_obs))
        rest = cell - lev * (lev_rows * total)
        row = jnp.zeros_like(rest)
        for level in range(1, lev_rows):
            row = row + (rest >= level * total).astype(jnp.int32)
        col = rest - row * total
        following = jnp.where(col + 1 == total, 0, col + 1)
        in_band = (rest >= 0) & (rest < lev_rows * total)
        for i, where in enumerate((col, following)):
            local = where - slab * cols
            mine = in_band & (local >= 0) & (local < cols)
            local = jnp.where(mine, local, 0)
            window = row * tiles + lax.shift_right_logical(local, 7)
            window = jnp.where(mine, window, -1)
            lane = local & (LANES - 1)
            for t in range(obs_tiles):
                at = slice(t * LANES, (t + 1) * LANES)
                keys[b, i, t, 0] = window[:, at]
                keys[b, i, t, 1] = lane[:, at]

    for b in range(n_blocks):
        locate(b)

    def gather(b, windows):
        for i in range(2):
            for t in range(obs_tiles):
                at = slice(t * LANES, (t + 1) * LANES)
                now = acc[i, :, at]
                window = keys[b, i, t, 0]
                lane = jnp.concatenate([keys[b, i, t, 1]] * (members // SUBLANES), axis=0)
                for ident, load in windows:
                    hit = jnp.concatenate([(window == ident).astype(jnp.int32)] * (members // SUBLANES), axis=0)
                    got = jnp.take_along_axis(load(), lane, axis=1, mode="promise_in_bounds")
                    now = jnp.where(hit > 0, got, now)
                acc[i, :, at] = now

    def finish_pick(b):
        frac = frac_ref[b : b + 1, :]
        value = acc[0] * (1.0 - frac) + acc[1] * frac
        pad = jnp.zeros((LANES - members, LANES), F32)
        for t in range(obs_tiles):
            at = slice(t * LANES, (t + 1) * LANES)
            part[b, at, :] = jnp.concatenate([value[:, at], pad], axis=0).T

    def pick_first(c, carry):
        windows = []
        for level in range(lev_rows):
            for w in range(wide):
                tile = c * wide + w
                load = lambda level=level, tile=tile: raw[:, level, pl.ds(pl.multiple_of(tile * LANES, LANES), LANES)]
                windows.append((level * tiles + tile, load))
        gather(0, windows)
        return carry

    def scatter(b, k):
        p, where = on_slab(k)
        return pltpu.make_async_remote_copy(
            src_ref=part.at[b, pl.ds(pl.multiple_of(p * slots, slots), slots), :], dst_ref=landed.at[b, k],
            send_sem=scat_send.at[b, k], recv_sem=scat_recv.at[b, k], device_id=where, device_id_type=MESH)

    def along(b, k):
        return pltpu.make_async_remote_copy(
            src_ref=zown.at[b], dst_ref=zland.at[b, k],
            send_sem=z_send.at[b, k], recv_sem=z_recv.at[b, k], device_id=on_line(k), device_id_type=MESH)

    def cast(b, k):
        return pltpu.make_async_remote_copy(
            src_ref=own.at[b], dst_ref=prior.at[b, slab],
            send_sem=cast_send.at[b, k], recv_sem=cast_recv.at[b, k], device_id=on_slab(k)[1], device_id_type=MESH)

    def exchange(b, fills):
        at, stop = 0, 0
        for k in range(1, n_slab):
            scatter(b, k).start()
        forwards(b, 0, fills[0])
        value = part[b, pl.ds(pl.multiple_of(slab * slots, slots), slots), :]
        for k in range(1, n_slab):
            scatter(b, k).wait_recv()
        for k in range(1, n_slab):
            value = value + landed[b, k]
        zown[b] = value
        for k in range(1, n_lev):
            along(b, k).start()
        forwards(b, fills[0], fills[0] + fills[1])
        for k in range(1, n_lev):
            along(b, k).wait_recv()
        for k in range(1, n_lev):
            value = value + zland[b, k]
        own[b] = value
        for k in range(1, n_slab):
            cast(b, k).start()
        prior[b, slab] = value
        forwards(b, fills[0] + fills[1], sum(fills))
        for k in range(1, n_slab):
            cast(b, k).wait_recv()

    def statistics(b):
        def column(ref):
            return jnp.broadcast_to(ref[b : b + 1, :], (SUBLANES, n_obs)).T[:, :1]

        value, var = column(value_ref), column(var_ref)
        now = prior[b].reshape(n_obs, LANES)
        live = lax.broadcasted_iota(jnp.int32, now.shape, 1) < members
        mean = jnp.sum(jnp.where(live, now, 0.0), axis=1, keepdims=True) / members
        deviation = jnp.where(live, now - mean, 0.0)
        spread = jnp.sum(deviation * deviation, axis=1, keepdims=True) / (members - 1.0)
        whole = spread + var
        shrink = 1.0 / (1.0 + jnp.sqrt(var / whole))
        gain = ((value - mean) - deviation * shrink) / (whole * (members - 1.0))
        dev_s[...] = deviation.astype(BF16)
        gain_s[...] = gain.T.astype(BF16)
        mean_ref[b : b + 1, :] = jnp.broadcast_to(mean, (n_obs, LANES)).T[:1, :]

    def spread_levels(b):
        for level in range(lev_rows):
            lev_s[level] = jnp.broadcast_to(lev_ref[b, level : level + 1, :], (LANES, n_obs)).T

    def update(b, c):
        first, last = b == 0, b == n_blocks - 1
        at = pl.ds(pl.multiple_of(c * width, width), width)
        dev = dev_s[:, :members]
        gain = gain_s[:members, :]
        loc = gat[b, :, at].astype(F32)
        for level in range(lev_rows):
            now = raw[:, level, at] if first else plain[level, :, at]
            centred = (now - jnp.sum(now, axis=0, keepdims=True) / members).astype(BF16)
            cross = jnp.dot(dev, centred, preferred_element_type=F32)
            height = jnp.concatenate([lev_s[level]] * wide, axis=1)
            mixed = ((height * loc) * cross).astype(BF16)
            new = now + jnp.dot(gain, mixed, preferred_element_type=F32)
            if last:
                raw[:, level, at] = new
            else:
                plain[level, :, at] = new
        if last:
            pltpu.make_async_copy(raw.at[:, :, at], out_ref.at[:, :, at], out_sem.at[c]).start()
        else:
            windows = []
            for level in range(lev_rows):
                for w in range(wide):
                    tile = c * wide + w
                    load = lambda level=level, tile=tile: plain[level, :, pl.ds(pl.multiple_of(tile * LANES, LANES), LANES)]
                    windows.append((level * tiles + tile, load))
            gather(b + 1, windows)

    acc[...] = jnp.zeros_like(acc)
    for load in loads[1:]:
        load.wait()
    lax.fori_loop(0, chunks, pick_first, 0)
    finish_pick(0)
    for b in range(n_blocks):
        fills = STEPS_FIRST if b == 0 else STEPS_LATER
        spread_levels(b)
        exchange(b, fills)
        statistics(b)
        if b + 1 < n_blocks:
            acc[...] = jnp.zeros_like(acc)
        done = sum(fills)
        early = max(done - lag, 0)

        def catch_up(c, carry):
            update(b, c)
            return carry

        def body(s, carry):
            forward(b, s)
            update(b, s - lag)
            return carry

        if early:
            lax.fori_loop(0, early, catch_up, 0)
        if done < lag:
            forwards(b, done, lag)
        lax.fori_loop(lag + early, steps, body, 0)
        if b + 1 < n_blocks:
            finish_pick(b + 1)

    def drain_first(c, carry):
        for way, step, alive in ends:
            @pl.when(alive)
            def _():
                hop(step, 0, lev, c, first_send.at[way, c]).wait_send()
        pltpu.make_async_copy(
            raw.at[:, :, pl.ds(pl.multiple_of(c * width, width), width)],
            out_ref.at[:, :, pl.ds(pl.multiple_of(c * width, width), width)], out_sem.at[c]).wait()
        return carry

    lax.fori_loop(0, chunks, drain_first, 0)
    for way, step, alive in ends:
        @pl.when(alive)
        def _():
            for d in range(n_lev - 1):
                if d == 0 and n_blocks == 1:
                    continue
                source = lev - step * d

                @pl.when((source >= 0) & (source < n_lev))
                def _():
                    for slot in range(2):
                        hop(step, 0, source, 0, line_send.at[way, d, slot]).wait_send()
    for b in range(n_blocks):
        for k in range(1, n_slab):
            scatter(b, k).wait_send()
            cast(b, k).wait_send()
        for k in range(1, n_lev):
            along(b, k).wait_send()


def analyse(n_slab, n_lev, ensemble, cells, values, variances, fracs, locs, heights):
    members, lev_rows, cols = ensemble.shape
    n_blocks, n_obs = cells.shape
    rows = locs.shape[1]
    width = next(t * LANES for t in (2, 1) if cols % (t * LANES) == 0)
    chunks = cols // width
    slots = n_obs // n_slab
    vmem = pl.BlockSpec(memory_space=pltpu.VMEM)
    hbm = pl.BlockSpec(memory_space=pltpu.HBM)
    dma = pltpu.SemaphoreType.DMA
    return pl.pallas_call(
        functools.partial(kernel, n_slab, n_lev),
        out_shape=[
            jax.ShapeDtypeStruct(ensemble.shape, F32),
            jax.ShapeDtypeStruct(values.shape, F32),
        ],
        in_specs=[vmem, vmem, vmem, vmem, vmem, hbm, hbm],
        out_specs=[pl.BlockSpec(memory_space=pl.ANY), vmem],
        scratch_shapes=[
            pltpu.VMEM((members, lev_rows, cols), F32),
            pltpu.VMEM((lev_rows, members, cols), F32),
            pltpu.VMEM((n_blocks, n_obs, cols), BF16),
            pltpu.VMEM((n_blocks, 2, n_obs // LANES, 2, SUBLANES, LANES), jnp.int32),
            pltpu.VMEM((2, members, n_obs), F32),
            pltpu.VMEM((n_blocks, n_obs, LANES), F32),
            pltpu.VMEM((n_blocks, n_slab, slots, LANES), F32),
            pltpu.VMEM((n_blocks, slots, LANES), F32),
            pltpu.VMEM((n_blocks, n_lev, slots, LANES), F32),
            pltpu.VMEM((n_blocks, slots, LANES), F32),
            pltpu.VMEM((n_blocks, n_slab, slots, LANES), F32),
            pltpu.VMEM((n_obs, LANES), BF16),
            pltpu.VMEM((LANES, n_obs), BF16),
            pltpu.VMEM((lev_rows, n_obs, LANES), F32),
            dma((n_blocks + 1,)),
            dma((n_blocks, n_lev, chunks)),
            dma((2, chunks)),
            dma((2, n_lev, 2)),
            dma((n_blocks, n_slab)),
            dma((n_blocks, n_slab)),
            dma((n_blocks, n_lev)),
            dma((n_blocks, n_lev)),
            dma((n_blocks, n_slab)),
            dma((n_blocks, n_slab)),
            dma((chunks,)),
        ],
        compiler_params=pltpu.CompilerParams(collective_id=0, has_side_effects=True, vmem_limit_bytes=28 << 20),
        name="analyse",
    )(cells, fracs, values, variances, heights, ensemble, locs)


def solution(mesh):
    n_slab, n_lev = mesh.shape["slab"], mesh.shape["lev"]

    def on_device(ensemble, obs_cell, obs_value, obs_var, obs_frac, loc_column, loc_level):
        heights = loc_level.transpose(0, 2, 1)
        state, means = analyse(n_slab, n_lev, ensemble, obs_cell, obs_value, obs_var, obs_frac, loc_column, heights)
        return state, means

    in_specs = (
        P(None, "lev", "slab"), P(), P(), P(), P(),
        P(None, "lev", "slab"), P(None, None, "lev"),
    )
    return jax.shard_map(
        on_device, mesh=mesh, in_specs=in_specs,
        out_specs=(P(None, "lev", "slab"), P()), check_vma=False,
    )
```

time: 101 us -> 73 us (0.72)
  Pallas kernels: 101 us -> 63.5 us
  local copies, waits for them, and re-layouts: 0 us -> 8.49 us
    pallas_call x6 -> x1, Pallas kernels: 101 us -> 63.5 us  [analyse(): pl.pallas_call(functools.partial(kernel, n_slab, n_lev), out_shape=[jax.S...]
    unnamed x0 -> x16, local copies, waits for them, and re-layouts: none -> 8.49 us
where the time goes in v1:
time: 73 us; the launch traced here: 72.6 us
  Pallas kernels  63.5 us (87%)
  local copies, waits for them, and re-layouts  8.49 us (12%)
    pallas_call x1, Pallas kernels, analyse(): pl.pallas_call(functools.partial(kernel, n_slab, n_lev), out_shape=[jax.S...  63.5 us
    unnamed x16, local copies, waits for them, and re-layouts  8.49 us

profile of v1, /device:TPU:0, one launch (start us, length us, event | category | flops | bytes accessed | tf_op | source)
XLA Modules:
  0.0 72.6 jit_solution(7862482819690172467)
XLA Ops:
  0.6 0.0 copy-start
  0.6 1.8 %copy-done = f32[80,4,2304]{2,1,0:T(4,128)S(1)} copy-done((f32[80,4,2304]{2,1,0:T(4,128)S(1)}, f32[80,4,2304]{2,1,0:T(4,128)}, u32[]{:S(2)}) %copy-start) | copy-done | bytes 2949144
  2.5 0.0 copy-start.1
  2.5 1.1 %copy-done.1 = bf16[2,64,2304]{2,1,0:T(8,128)(2,1)S(1)} copy-done((bf16[2,64,2304]{2,1,0:T(8,128)(2,1)S(1)}, bf16[2,64,2304]{2,1,0:T(8,128)(2,1)}, u32[]{:S(2)}) %copy-start.1) | copy-done | bytes 589848
  3.5 0.0 copy-start.2
  3.5 0.7 copy-done.2
  4.2 0.0 copy-start.3
  4.2 0.7 copy-done.3
  4.9 0.0 copy-start.4
  4.9 0.7 copy-done.4
  5.6 0.0 copy-start.5
  5.6 0.7 copy-done.5
  6.3 0.0 copy-start.6
  6.3 0.7 copy-done.6
  7.0 63.5 %analyse.1 = (f32[80,4,2304]{2,1,0:T(4,128)S(1)}, f32[2,256]{1,0:T(2,128)S(1)}) custom-call(s32[2,256]{1,0:T(2,128)S(1)} %copy-done.3, f32[2,256]{1,0:T(2,128)S(1)} %copy-done.4, f32[2,256]{1,0:T(2,128)S(1)} %copy-done.5, f32[2,256]{1,0:T(2,128)S(1)} %copy-done.6, f32[2,4,256]{2,1,0:T(4,128)S(1)} %bitcast.1, f32[80,4,2304]{2,1,0:T(4,128)S(1)} %copy-done, ...), custom_call_target="tpu_custom_call" | custom-call | tf_op jit(solution)/shard_map/analyse/pallas_call | solution.py:344
  70.4 1.6 %copy.11 = f32[80,4,2304]{2,1,0:T(4,128)} copy(f32[80,4,2304]{2,1,0:T(4,128)S(1)} %get-tuple-element.4) | data formatting | bytes 5898240
  72.0 0.6 copy.12
Async XLA Ops:
  0.6 1.8 %copy-start = (f32[80,4,2304]{2,1,0:T(4,128)S(1)}, f32[80,4,2304]{2,1,0:T(4,128)}, u32[]{:S(2)}) copy-start(f32[80,4,2304]{2,1,0:T(4,128)} %ens_hbm.1) | copy-start | bytes 8847364
  2.5 1.1 %copy-start.1 = (bf16[2,64,2304]{2,1,0:T(8,128)(2,1)S(1)}, bf16[2,64,2304]{2,1,0:T(8,128)(2,1)}, u32[]{:S(2)}) copy-start(bf16[2,64,2304]{2,1,0:T(8,128)(2,1)} %loc_hbm.1) | copy-start | bytes 1769476
  3.5 0.7 copy-start.2
  4.2 0.7 copy-start.3
  4.9 0.7 copy-start.4
  5.6 0.7 copy-start.5
  6.3 0.7 copy-start.6

commit v2 on v1

--- a/solution.py
+++ b/solution.py
@@ -13,17 +13,17 @@
 F32 = jnp.float32
 BF16 = jnp.bfloat16
 SKEW = 3
-STEPS_FIRST = (1, 2, 1)
-STEPS_LATER = (2, 3, 2)
+STEPS_FIRST = (3,3,3)
+STEPS_LATER = (3,3,3)
 
 
 def kernel(
-    n_slab, n_lev, cell_ref, frac_ref, value_ref, var_ref, lev_ref, ens_hbm, loc_hbm, out_ref, mean_ref,
-    raw, plain, gat, keys, acc, part, landed, zown, zland, own, prior, dev_s, gain_s, lev_s,
-    load_sem, line_recv, first_send, line_send, scat_send, scat_recv, z_send, z_recv, cast_send, cast_recv, out_sem,
+    n_slab, n_lev, cell_hbm, frac_hbm, value_hbm, var_hbm, lev_hbm, ens_hbm, loc_hbm, state, mean_ref,
+    cell_ref, frac_ref, value_ref, var_ref, lev_ref, gat, keys, acc, part, landed, zown, zland, own, prior, dev_s, gain_s, lev_s,
+    load_sem, line_recv, first_send, line_send, scat_send, scat_recv, z_send, z_recv, cast_send, cast_recv,
 ):
-    members, lev_rows, cols = raw.shape
-    n_blocks, n_obs = cell_ref.shape
+    lev_rows, members, cols = state.shape
+    n_blocks, n_obs = cell_hbm.shape
     rows = loc_hbm.shape[1]
     tiles = cols // LANES
     chunks = line_recv.shape[2]
@@ -40,7 +40,10 @@
         pltpu.make_async_copy(loc_hbm.at[b], gat.at[b, pl.ds(pl.multiple_of(lev * rows, rows), rows), :], load_sem.at[b])
         for b in range(n_blocks)
     ]
-    loads.append(pltpu.make_async_copy(ens_hbm, raw, load_sem.at[n_blocks]))
+    small = ((cell_hbm, cell_ref), (frac_hbm, frac_ref), (value_hbm, value_ref), (var_hbm, var_ref), (lev_hbm, lev_ref))
+    small += tuple((ens_hbm.at[:, level, :], state.at[level]) for level in range(lev_rows))
+    for i, (src, dst) in enumerate(small):
+        loads.append(pltpu.make_async_copy(src, dst, load_sem.at[n_blocks + i]))
     for load in loads:
         load.start()
 
@@ -88,8 +91,6 @@
         hop(step, b, source, c, sem).start()
 
     def forward(b, s):
-        if b + 1 < n_blocks:
-            pass
         for d in range(1, n_lev):
             c = s - (d - 1) * SKEW
 
@@ -143,20 +144,22 @@
                 keys[b, i, t, 0] = window[:, at]
                 keys[b, i, t, 1] = lane[:, at]
 
-    for b in range(n_blocks):
-        locate(b)
-
-    def gather(b, windows):
+
+    def gather(b, c):
         for i in range(2):
             for t in range(obs_tiles):
                 at = slice(t * LANES, (t + 1) * LANES)
                 now = acc[i, :, at]
                 window = keys[b, i, t, 0]
                 lane = jnp.concatenate([keys[b, i, t, 1]] * (members // SUBLANES), axis=0)
-                for ident, load in windows:
-                    hit = jnp.concatenate([(window == ident).astype(jnp.int32)] * (members // SUBLANES), axis=0)
-                    got = jnp.take_along_axis(load(), lane, axis=1, mode="promise_in_bounds")
-                    now = jnp.where(hit > 0, got, now)
+                for level in range(lev_rows):
+                    for w in range(wide):
+                        tile = c * wide + w
+                        hit = (window == level * tiles + tile).astype(jnp.int32)
+                        hit = jnp.concatenate([hit] * (members // SUBLANES), axis=0)
+                        held = state[level, :, pl.ds(pl.multiple_of(tile * LANES, LANES), LANES)]
+                        got = jnp.take_along_axis(held, lane, axis=1, mode="promise_in_bounds")
+                        now = jnp.where(hit > 0, got, now)
                 acc[i, :, at] = now
 
     def finish_pick(b):
@@ -168,13 +171,7 @@
             part[b, at, :] = jnp.concatenate([value[:, at], pad], axis=0).T
 
     def pick_first(c, carry):
-        windows = []
-        for level in range(lev_rows):
-            for w in range(wide):
-                tile = c * wide + w
-                load = lambda level=level, tile=tile: raw[:, level, pl.ds(pl.multiple_of(tile * LANES, LANES), LANES)]
-                windows.append((level * tiles + tile, load))
-        gather(0, windows)
+        gather(0, c)
         return carry
 
     def scatter(b, k):
@@ -194,7 +191,6 @@
             send_sem=cast_send.at[b, k], recv_sem=cast_recv.at[b, k], device_id=on_slab(k)[1], device_id_type=MESH)
 
     def exchange(b, fills):
-        at, stop = 0, 0
         for k in range(1, n_slab):
             scatter(b, k).start()
         forwards(b, 0, fills[0])
@@ -241,36 +237,27 @@
             lev_s[level] = jnp.broadcast_to(lev_ref[b, level : level + 1, :], (LANES, n_obs)).T
 
     def update(b, c):
-        first, last = b == 0, b == n_blocks - 1
         at = pl.ds(pl.multiple_of(c * width, width), width)
         dev = dev_s[:, :members]
         gain = gain_s[:members, :]
         loc = gat[b, :, at].astype(F32)
-        for level in range(lev_rows):
-            now = raw[:, level, at] if first else plain[level, :, at]
-            centred = (now - jnp.sum(now, axis=0, keepdims=True) / members).astype(BF16)
-            cross = jnp.dot(dev, centred, preferred_element_type=F32)
-            height = jnp.concatenate([lev_s[level]] * wide, axis=1)
-            mixed = ((height * loc) * cross).astype(BF16)
-            new = now + jnp.dot(gain, mixed, preferred_element_type=F32)
-            if last:
-                raw[:, level, at] = new
-            else:
-                plain[level, :, at] = new
-        if last:
-            pltpu.make_async_copy(raw.at[:, :, at], out_ref.at[:, :, at], out_sem.at[c]).start()
-        else:
-            windows = []
-            for level in range(lev_rows):
-                for w in range(wide):
-                    tile = c * wide + w
-                    load = lambda level=level, tile=tile: plain[level, :, pl.ds(pl.multiple_of(tile * LANES, LANES), LANES)]
-                    windows.append((level * tiles + tile, load))
-            gather(b + 1, windows)
+        levels = range(lev_rows)
+        now = [state[level, :, at] for level in levels]
+        centred = [(x - jnp.sum(x, axis=0, keepdims=True) / members).astype(BF16) for x in now]
+        cross = [jnp.dot(dev, x, preferred_element_type=F32) for x in centred]
+        height = [jnp.concatenate([lev_s[level]] * wide, axis=1) for level in levels]
+        mixed = [((height[level] * loc) * cross[level]).astype(BF16) for level in levels]
+        new = [now[level] + jnp.dot(gain, mixed[level], preferred_element_type=F32) for level in levels]
+        for level in levels:
+            state[level, :, at] = new[level]
+        if b + 1 < n_blocks:
+            gather(b + 1, c)
 
     acc[...] = jnp.zeros_like(acc)
     for load in loads[1:]:
         load.wait()
+    for b in range(n_blocks):
+        locate(b)
     lax.fori_loop(0, chunks, pick_first, 0)
     finish_pick(0)
     for b in range(n_blocks):
@@ -283,20 +270,20 @@
         done = sum(fills)
         early = max(done - lag, 0)
 
-        def catch_up(c, carry):
-            update(b, c)
+        def double(s, carry):
+            forward(b, s)
+            update(b, 2 * (s - done))
+            update(b, 2 * (s - done) + 1)
             return carry
 
-        def body(s, carry):
+        def single(s, carry):
             forward(b, s)
             update(b, s - lag)
             return carry
 
-        if early:
-            lax.fori_loop(0, early, catch_up, 0)
-        if done < lag:
-            forwards(b, done, lag)
-        lax.fori_loop(lag + early, steps, body, 0)
+        forwards(b, done, lag)
+        lax.fori_loop(lag + early, lag + 2 * early, double, 0)
+        lax.fori_loop(lag + 2 * early, steps, single, 0)
         if b + 1 < n_blocks:
             finish_pick(b + 1)
 
@@ -305,9 +292,6 @@
             @pl.when(alive)
             def _():
                 hop(step, 0, lev, c, first_send.at[way, c]).wait_send()
-        pltpu.make_async_copy(
-            raw.at[:, :, pl.ds(pl.multiple_of(c * width, width), width)],
-            out_ref.at[:, :, pl.ds(pl.multiple_of(c * width, width), width)], out_sem.at[c]).wait()
         return carry
 
     lax.fori_loop(0, chunks, drain_first, 0)
@@ -344,14 +328,17 @@
     return pl.pallas_call(
         functools.partial(kernel, n_slab, n_lev),
         out_shape=[
-            jax.ShapeDtypeStruct(ensemble.shape, F32),
-            jax.ShapeDtypeStruct(values.shape, F32),
+            pltpu.VMEM((lev_rows, members, cols), F32),
+            pltpu.VMEM(values.shape, F32),
         ],
-        in_specs=[vmem, vmem, vmem, vmem, vmem, hbm, hbm],
-        out_specs=[pl.BlockSpec(memory_space=pl.ANY), vmem],
+        in_specs=[hbm] * 7,
+        out_specs=[vmem, vmem],
         scratch_shapes=[
-            pltpu.VMEM((members, lev_rows, cols), F32),
-            pltpu.VMEM((lev_rows, members, cols), F32),
+            pltpu.VMEM(cells.shape, jnp.int32),
+            pltpu.VMEM(fracs.shape, F32),
+            pltpu.VMEM(values.shape, F32),
+            pltpu.VMEM(variances.shape, F32),
+            pltpu.VMEM(heights.shape, F32),
             pltpu.VMEM((n_blocks, n_obs, cols), BF16),
             pltpu.VMEM((n_blocks, 2, n_obs // LANES, 2, SUBLANES, LANES), jnp.int32),
             pltpu.VMEM((2, members, n_obs), F32),
@@ -364,7 +351,7 @@
             pltpu.VMEM((n_obs, LANES), BF16),
             pltpu.VMEM((LANES, n_obs), BF16),
             pltpu.VMEM((lev_rows, n_obs, LANES), F32),
-            dma((n_blocks + 1,)),
+            dma((n_blocks + 5 + lev_rows,)),
             dma((n_blocks, n_lev, chunks)),
             dma((2, chunks)),
             dma((2, n_lev, 2)),
@@ -374,11 +361,35 @@
             dma((n_blocks, n_lev)),
             dma((n_blocks, n_slab)),
             dma((n_blocks, n_slab)),
-            dma((chunks,)),
         ],
         compiler_params=pltpu.CompilerParams(collective_id=0, has_side_effects=True, vmem_limit_bytes=28 << 20),
         name="analyse",
-    )(cells, fracs, values, variances, heights, ensemble, locs)
+    )(*(pltpu.with_memory_space_constraint(x, pltpu.HBM) for x in (cells, fracs, values, variances, heights, ensemble, locs)))
+
+
+def hand_over_kernel(state, means, out_ref, mean_ref, sem):
+    lev_rows = state.shape[0]
+    copies = [pltpu.make_async_copy(state.at[level], out_ref.at[:, level, :], sem.at[level]) for level in range(lev_rows)]
+    copies.append(pltpu.make_async_copy(means, mean_ref, sem.at[lev_rows]))
+    for copy in copies:
+        copy.start()
+    for copy in copies:
+        copy.wait()
+
+
+def hand_over(state, means):
+    lev_rows, members, cols = state.shape
+    vmem = pl.BlockSpec(memory_space=pltpu.VMEM)
+    hbm = pl.BlockSpec(memory_space=pltpu.HBM)
+    return pl.pallas_call(
+        hand_over_kernel,
+        out_shape=[pltpu.HBM((members, lev_rows, cols), F32), pltpu.HBM(means.shape, F32)],
+        in_specs=[vmem, vmem],
+        out_specs=[hbm, hbm],
+        scratch_shapes=[pltpu.SemaphoreType.DMA((lev_rows + 1,))],
+        compiler_params=pltpu.CompilerParams(vmem_limit_bytes=8 << 20),
+        name="hand_over",
+    )(*(pltpu.with_memory_space_constraint(x, pltpu.VMEM) for x in (state, means)))
 
 
 def solution(mesh):
@@ -387,7 +398,7 @@
     def on_device(ensemble, obs_cell, obs_value, obs_var, obs_frac, loc_column, loc_level):
         heights = loc_level.transpose(0, 2, 1)
         state, means = analyse(n_slab, n_lev, ensemble, obs_cell, obs_value, obs_var, obs_frac, loc_column, heights)
-        return state, means
+        return tuple(hand_over(state, means))
 
     in_specs = (
         P(None, "lev", "slab"), P(), P(), P(), P(),

time: 73 us -> 52.7 us (0.72)
  Pallas kernels: 63.5 us -> 51.9 us
  local copies, waits for them, and re-layouts: 8.49 us -> 0 us
    pallas_call x1 -> x2, Pallas kernels: 63.5 us -> 51.9 us  [the longest x1 50.3 us: analyse(): pl.pallas_call(functools.partial(kernel, n_slab, n_lev), out_shape=[pltpu...]
    unnamed x16 -> x0, local copies, waits for them, and re-layouts: 8.49 us -> none
where the time goes in v2:
time: 52.7 us; the launch traced here: 52.6 us
  Pallas kernels  51.9 us (98%)
  between operations  0.64 us (1%)
    pallas_call x1, Pallas kernels, analyse(): pl.pallas_call(functools.partial(kernel, n_slab, n_lev), out_shape=[pltpu...  50.3 us
    pallas_call x1, Pallas kernels, hand_over(): pl.pallas_call(hand_over_kernel, out_shape=[pltpu.HBM((members, lev_rows,...  1.64 us

profile of v2, /device:TPU:0, one launch (start us, length us, event | category | flops | bytes accessed | tf_op | source)
XLA Modules:
  0.0 52.6 jit_solution(12427977401051080549)
XLA Ops:
  0.6 50.3 %analyse.1 = (f32[4,80,2304]{2,1,0:T(8,128)S(1)}, f32[2,256]{1,0:T(2,128)S(1)}) custom-call(s32[2,256]{1,0:T(2,128)} %cell_hbm.1, f32[2,256]{1,0:T(2,128)} %frac_hbm.1, f32[2,256]{1,0:T(2,128)} %value_hbm.1, f32[2,256]{1,0:T(2,128)} %var_hbm.1, f32[2,4,256]{2,1,0:T(4,128)} %bitcast.1, f32[80,4,2304]{2,1,0:T(4,128)} %ens_hbm.1, bf16[2,64,2304]{2,1,0:T(8,128)(2,1)} %loc_hbm.1), custom_call_target="tpu_custom_call" | custom-call | tf_op jit(solution)/shard_map/analyse/pallas_call | solution.py:328
  50.9 1.6 %hand_over.1 = (f32[80,4,2304]{2,1,0:T(4,128)}, f32[2,256]{1,0:T(2,128)}) custom-call(f32[4,80,2304]{2,1,0:T(8,128)S(1)} %get-tuple-element.4.state, f32[2,256]{1,0:T(2,128)S(1)} %get-tuple-element.5.means), custom_call_target="tpu_custom_call" | custom-call | tf_op jit(solution)/shard_map/hand_over/pallas_call | solution.py:384

commit v3 on v2

--- a/solution.py
+++ b/solution.py
@@ -13,14 +13,14 @@
 F32 = jnp.float32
 BF16 = jnp.bfloat16
 SKEW = 3
-STEPS_FIRST = (3,3,3)
-STEPS_LATER = (3,3,3)
+STEPS_FIRST = (3, 3, 2)
+STEPS_LATER = (4, 3, 2)
 
 
 def kernel(
     n_slab, n_lev, cell_hbm, frac_hbm, value_hbm, var_hbm, lev_hbm, ens_hbm, loc_hbm, state, mean_ref,
     cell_ref, frac_ref, value_ref, var_ref, lev_ref, gat, keys, acc, part, landed, zown, zland, own, prior, dev_s, gain_s, lev_s,
-    load_sem, line_recv, first_send, line_send, scat_send, scat_recv, z_send, z_recv, cast_send, cast_recv,
+    load_sem, line_recv, own_send, line_send, scat_send, scat_recv, z_send, z_recv, cast_send, cast_recv,
 ):
     lev_rows, members, cols = state.shape
     n_blocks, n_obs = cell_hbm.shape
@@ -30,21 +30,22 @@
     width = cols // chunks
     wide = width // LANES
     total = cols * n_slab
-    slots = n_obs // n_slab
+    slots = own.shape[1]
     lag = SKEW * (n_lev - 2)
     steps = chunks + lag
     obs_tiles = n_obs // LANES
     slab, lev = lax.axis_index("slab"), lax.axis_index("lev")
 
-    loads = [
-        pltpu.make_async_copy(loc_hbm.at[b], gat.at[b, pl.ds(pl.multiple_of(lev * rows, rows), rows), :], load_sem.at[b])
-        for b in range(n_blocks)
-    ]
+    mine = pl.ds(pl.multiple_of(lev * rows, rows), rows)
     small = ((cell_hbm, cell_ref), (frac_hbm, frac_ref), (value_hbm, value_ref), (var_hbm, var_ref), (lev_hbm, lev_ref))
-    small += tuple((ens_hbm.at[:, level, :], state.at[level]) for level in range(lev_rows))
-    for i, (src, dst) in enumerate(small):
-        loads.append(pltpu.make_async_copy(src, dst, load_sem.at[n_blocks + i]))
-    for load in loads:
+    loads = [(loc_hbm.at[b], gat.at[b, mine, :]) for b in range(n_blocks)] + list(small)
+    loads = [pltpu.make_async_copy(src, dst, load_sem.at[i]) for i, (src, dst) in enumerate(loads)]
+    state_sem = load_sem.at[len(loads)]
+    for load in loads[:n_blocks]:
+        load.start()
+    for level in range(lev_rows):
+        pltpu.make_async_copy(ens_hbm.at[:, level, :], state.at[level], state_sem).start()
+    for load in loads[n_blocks:]:
         load.start()
 
     def on_slab(k):
@@ -65,24 +66,37 @@
         spot = gat.at[
             b, pl.ds(pl.multiple_of(source * rows, rows), rows), pl.ds(pl.multiple_of(c * width, width), width)
         ]
-        return pltpu.make_async_remote_copy(
-            src_ref=spot, dst_ref=spot, send_sem=sem, recv_sem=line_recv.at[b, source, c],
-            device_id=(slab, lev + step), device_id_type=MESH)
+        there = lev + step
+        slot = source - (source > there).astype(jnp.int32)
+        return pltpu.make_async_remote_copy(
+            src_ref=spot, dst_ref=spot, send_sem=sem, recv_sem=line_recv.at[b, slot, c],
+            device_id=(slab, there), device_id_type=MESH)
+
+    def landing(b, source, c, sem):
+        slot = source - (source > lev).astype(jnp.int32)
+        spot = gat.at[
+            b, pl.ds(pl.multiple_of(source * rows, rows), rows), pl.ds(pl.multiple_of(c * width, width), width)
+        ]
+        return pltpu.make_async_remote_copy(
+            src_ref=spot, dst_ref=spot, send_sem=sem, recv_sem=line_recv.at[b, slot, c],
+            device_id=(slab, lev), device_id_type=MESH)
 
     ends = ((0, 1, lev < n_lev - 1), (1, -1, lev > 0))
 
-    def send_own_first(c, carry):
-        for way, step, alive in ends:
-            @pl.when(alive)
-            def _():
-                hop(step, 0, lev, c, first_send.at[way, c]).start()
-        return carry
+    def send_own(b):
+        def body(c, carry):
+            for way, step, alive in ends:
+                @pl.when(alive)
+                def _():
+                    hop(step, b, lev, c, own_send.at[b, way]).start()
+            return carry
+        lax.fori_loop(0, chunks, body, 0)
 
     loads[0].wait()
-    lax.fori_loop(0, chunks, send_own_first, 0)
+    send_own(0)
 
     def send(way, step, d, b, source, c, order):
-        sem = line_send.at[way, d, lax.rem(order, 2)]
+        sem = line_send.at[way, d - 1, lax.rem(order, 2)]
 
         @pl.when(order >= 2)
         def _():
@@ -101,21 +115,11 @@
 
                     @pl.when((source >= 0) & (source < n_lev))
                     def _():
-                        hop(step, b, source, c, line_send.at[way, d, 0]).wait_recv()
+                        landing(b, source, c, line_send.at[way, 0, 0]).wait_recv()
                         if d < n_lev - 1:
                             @pl.when(alive)
                             def _():
                                 send(way, step, d, b, source, c, c + b * chunks)
-
-        for nxt in range(1, n_blocks):
-            c = s + (b - nxt + 1) * steps - chunks
-
-            @pl.when((c >= 0) & (c < chunks))
-            def _():
-                for way, step, alive in ends:
-                    @pl.when(alive)
-                    def _():
-                        send(way, step, 0, nxt, lev, c, c + (nxt - 1) * chunks)
 
     def forwards(b, start, stop):
         def body(s, carry):
@@ -165,10 +169,8 @@
     def finish_pick(b):
         frac = frac_ref[b : b + 1, :]
         value = acc[0] * (1.0 - frac) + acc[1] * frac
-        pad = jnp.zeros((LANES - members, LANES), F32)
         for t in range(obs_tiles):
-            at = slice(t * LANES, (t + 1) * LANES)
-            part[b, at, :] = jnp.concatenate([value[:, at], pad], axis=0).T
+            part[b, t * members : (t + 1) * members, :] = value[:, t * LANES : (t + 1) * LANES]
 
     def pick_first(c, carry):
         gather(0, c)
@@ -177,8 +179,19 @@
     def scatter(b, k):
         p, where = on_slab(k)
         return pltpu.make_async_remote_copy(
-            src_ref=part.at[b, pl.ds(pl.multiple_of(p * slots, slots), slots), :], dst_ref=landed.at[b, k],
-            send_sem=scat_send.at[b, k], recv_sem=scat_recv.at[b, k], device_id=where, device_id_type=MESH)
+            src_ref=part.at[b, pl.ds(pl.multiple_of(p * slots, slots), slots), :], dst_ref=landed.at[b, k - 1],
+            send_sem=scat_send.at[b], recv_sem=scat_recv.at[b], device_id=where, device_id_type=MESH)
+
+    def scattered(b):
+        return pltpu.make_async_remote_copy(
+            src_ref=landed.at[b], dst_ref=landed.at[b],
+            send_sem=scat_send.at[b], recv_sem=scat_recv.at[b], device_id=on_slab(1)[1], device_id_type=MESH)
+
+    def collected(b):
+        some = prior.at[b, pl.ds(0, n_slab - 1)]
+        return pltpu.make_async_remote_copy(
+            src_ref=some, dst_ref=some,
+            send_sem=cast_send.at[b], recv_sem=cast_recv.at[b], device_id=on_slab(1)[1], device_id_type=MESH)
 
     def along(b, k):
         return pltpu.make_async_remote_copy(
@@ -188,16 +201,15 @@
     def cast(b, k):
         return pltpu.make_async_remote_copy(
             src_ref=own.at[b], dst_ref=prior.at[b, slab],
-            send_sem=cast_send.at[b, k], recv_sem=cast_recv.at[b, k], device_id=on_slab(k)[1], device_id_type=MESH)
+            send_sem=cast_send.at[b], recv_sem=cast_recv.at[b], device_id=on_slab(k)[1], device_id_type=MESH)
 
     def exchange(b, fills):
         for k in range(1, n_slab):
             scatter(b, k).start()
         forwards(b, 0, fills[0])
         value = part[b, pl.ds(pl.multiple_of(slab * slots, slots), slots), :]
-        for k in range(1, n_slab):
-            scatter(b, k).wait_recv()
-        for k in range(1, n_slab):
+        scattered(b).wait_recv()
+        for k in range(n_slab - 1):
             value = value + landed[b, k]
         zown[b] = value
         for k in range(1, n_lev):
@@ -212,25 +224,22 @@
             cast(b, k).start()
         prior[b, slab] = value
         forwards(b, fills[0] + fills[1], sum(fills))
-        for k in range(1, n_slab):
-            cast(b, k).wait_recv()
+        collected(b).wait_recv()
 
     def statistics(b):
-        def column(ref):
-            return jnp.broadcast_to(ref[b : b + 1, :], (SUBLANES, n_obs)).T[:, :1]
-
-        value, var = column(value_ref), column(var_ref)
-        now = prior[b].reshape(n_obs, LANES)
-        live = lax.broadcasted_iota(jnp.int32, now.shape, 1) < members
-        mean = jnp.sum(jnp.where(live, now, 0.0), axis=1, keepdims=True) / members
-        deviation = jnp.where(live, now - mean, 0.0)
-        spread = jnp.sum(deviation * deviation, axis=1, keepdims=True) / (members - 1.0)
+        now = prior[b].reshape(n_slab * slots, LANES)
+        now = jnp.concatenate([now[t * members : (t + 1) * members] for t in range(obs_tiles)], axis=1)
+        value, var = value_ref[b : b + 1, :], var_ref[b : b + 1, :]
+        mean = jnp.sum(now, axis=0, keepdims=True) / members
+        deviation = now - mean
+        spread = jnp.sum(deviation * deviation, axis=0, keepdims=True) / (members - 1.0)
         whole = spread + var
         shrink = 1.0 / (1.0 + jnp.sqrt(var / whole))
         gain = ((value - mean) - deviation * shrink) / (whole * (members - 1.0))
-        dev_s[...] = deviation.astype(BF16)
-        gain_s[...] = gain.T.astype(BF16)
-        mean_ref[b : b + 1, :] = jnp.broadcast_to(mean, (n_obs, LANES)).T[:1, :]
+        pad = jnp.zeros((LANES - members, n_obs), F32)
+        dev_s[...] = jnp.concatenate([deviation, pad], axis=0).T.astype(BF16)
+        gain_s[...] = gain.astype(BF16)
+        mean_ref[b : b + 1, :] = mean
 
     def spread_levels(b):
         for level in range(lev_rows):
@@ -239,7 +248,7 @@
     def update(b, c):
         at = pl.ds(pl.multiple_of(c * width, width), width)
         dev = dev_s[:, :members]
-        gain = gain_s[:members, :]
+        gain = gain_s[...]
         loc = gat[b, :, at].astype(F32)
         levels = range(lev_rows)
         now = [state[level, :, at] for level in levels]
@@ -250,12 +259,11 @@
         new = [now[level] + jnp.dot(gain, mixed[level], preferred_element_type=F32) for level in levels]
         for level in levels:
             state[level, :, at] = new[level]
-        if b + 1 < n_blocks:
-            gather(b + 1, c)
-
     acc[...] = jnp.zeros_like(acc)
+    part[...] = jnp.zeros_like(part)
     for load in loads[1:]:
         load.wait()
+    pltpu.make_async_copy(state, state, state_sem).wait()
     for b in range(n_blocks):
         locate(b)
     lax.fori_loop(0, chunks, pick_first, 0)
@@ -270,6 +278,15 @@
         done = sum(fills)
         early = max(done - lag, 0)
 
+        def advance(c):
+            if b + 1 < n_blocks:
+                gather(b + 1, c - 1)
+            update(b, c)
+
+        def plain(c, carry):
+            advance(c)
+            return carry
+
         def double(s, carry):
             forward(b, s)
             update(b, 2 * (s - done))
@@ -278,39 +295,52 @@
 
         def single(s, carry):
             forward(b, s)
-            update(b, s - lag)
+            advance(s - lag)
             return carry
 
-        forwards(b, done, lag)
-        lax.fori_loop(lag + early, lag + 2 * early, double, 0)
-        lax.fori_loop(lag + 2 * early, steps, single, 0)
+        if b + 1 < n_blocks:
+            sent = steps - SKEW
+
+            forwards(b, done, lag + 1)
+            base = max(done, lag + 1)
+            forward(b, base)
+            update(b, 0)
+
+            def between(s, carry):
+                forward(b, s)
+                advance(s - base)
+                return carry
+
+            lax.fori_loop(base + 1, sent, between, 0)
+            send_own(b + 1)
+            lax.fori_loop(sent - base, sent - lag, plain, 0)
+            lax.fori_loop(sent, steps, single, 0)
+            gather(b + 1, chunks - 1)
+        else:
+            forwards(b, done, lag)
+            lax.fori_loop(lag + early, lag + 2 * early, double, 0)
+            lax.fori_loop(lag + 2 * early, steps, single, 0)
         if b + 1 < n_blocks:
             finish_pick(b + 1)
 
-    def drain_first(c, carry):
-        for way, step, alive in ends:
-            @pl.when(alive)
-            def _():
-                hop(step, 0, lev, c, first_send.at[way, c]).wait_send()
-        return carry
-
-    lax.fori_loop(0, chunks, drain_first, 0)
     for way, step, alive in ends:
         @pl.when(alive)
         def _():
-            for d in range(n_lev - 1):
-                if d == 0 and n_blocks == 1:
-                    continue
+            for b in range(n_blocks):
+                whole = gat.at[b, mine, :]
+                pltpu.make_async_remote_copy(
+                    src_ref=whole, dst_ref=whole, send_sem=own_send.at[b, way], recv_sem=line_recv.at[0, 0, 0],
+                    device_id=(slab, lev + step), device_id_type=MESH).wait_send()
+            for d in range(1, n_lev - 1):
                 source = lev - step * d
 
                 @pl.when((source >= 0) & (source < n_lev))
                 def _():
                     for slot in range(2):
-                        hop(step, 0, source, 0, line_send.at[way, d, slot]).wait_send()
+                        hop(step, 0, source, 0, line_send.at[way, d - 1, slot]).wait_send()
     for b in range(n_blocks):
-        for k in range(1, n_slab):
-            scatter(b, k).wait_send()
-            cast(b, k).wait_send()
+        scattered(b).wait_send()
+        collected(b).wait_send()
         for k in range(1, n_lev):
             along(b, k).wait_send()
 
@@ -321,7 +351,8 @@
     rows = locs.shape[1]
     width = next(t * LANES for t in (2, 1) if cols % (t * LANES) == 0)
     chunks = cols // width
-    slots = n_obs // n_slab
+    packed = members * (n_obs // LANES)
+    slots = pl.cdiv(packed, n_slab * SUBLANES) * SUBLANES
     vmem = pl.BlockSpec(memory_space=pltpu.VMEM)
     hbm = pl.BlockSpec(memory_space=pltpu.HBM)
     dma = pltpu.SemaphoreType.DMA
@@ -342,25 +373,25 @@
             pltpu.VMEM((n_blocks, n_obs, cols), BF16),
             pltpu.VMEM((n_blocks, 2, n_obs // LANES, 2, SUBLANES, LANES), jnp.int32),
             pltpu.VMEM((2, members, n_obs), F32),
-            pltpu.VMEM((n_blocks, n_obs, LANES), F32),
-            pltpu.VMEM((n_blocks, n_slab, slots, LANES), F32),
+            pltpu.VMEM((n_blocks, n_slab * slots, LANES), F32),
+            pltpu.VMEM((n_blocks, n_slab - 1, slots, LANES), F32),
             pltpu.VMEM((n_blocks, slots, LANES), F32),
             pltpu.VMEM((n_blocks, n_lev, slots, LANES), F32),
             pltpu.VMEM((n_blocks, slots, LANES), F32),
             pltpu.VMEM((n_blocks, n_slab, slots, LANES), F32),
             pltpu.VMEM((n_obs, LANES), BF16),
-            pltpu.VMEM((LANES, n_obs), BF16),
+            pltpu.VMEM((members, n_obs), BF16),
             pltpu.VMEM((lev_rows, n_obs, LANES), F32),
-            dma((n_blocks + 5 + lev_rows,)),
-            dma((n_blocks, n_lev, chunks)),
-            dma((2, chunks)),
-            dma((2, n_lev, 2)),
-            dma((n_blocks, n_slab)),
-            dma((n_blocks, n_slab)),
+            dma((n_blocks + 6,)),
+            dma((n_blocks, n_lev - 1, chunks)),
+            dma((n_blocks, 2)),
+            dma((2, n_lev - 2, 2)),
+            dma((n_blocks,)),
+            dma((n_blocks,)),
             dma((n_blocks, n_lev)),
             dma((n_blocks, n_lev)),
-            dma((n_blocks, n_slab)),
-            dma((n_blocks, n_slab)),
+            dma((n_blocks,)),
+            dma((n_blocks,)),
         ],
         compiler_params=pltpu.CompilerParams(collective_id=0, has_side_effects=True, vmem_limit_bytes=28 << 20),
         name="analyse",

time: 52.7 us -> 50.7 us (0.962)
  Pallas kernels: 51.9 us -> 49.9 us
    pallas_call x1, Pallas kernels: 50.3 us -> 48.3 us  [analyse(): pl.pallas_call(functools.partial(kernel, n_slab, n_lev), out_shape=[pltpu...]
where the time goes in v3:
time: 50.7 us; the launch traced here: 50.6 us
  Pallas kernels  49.9 us (98%)
  between operations  0.64 us (1%)
    pallas_call x1, Pallas kernels, analyse(): pl.pallas_call(functools.partial(kernel, n_slab, n_lev), out_shape=[pltpu...  48.3 us
    pallas_call x1, Pallas kernels, hand_over(): pl.pallas_call(hand_over_kernel, out_shape=[pltpu.HBM((members, lev_rows,...  1.64 us

profile of v3, /device:TPU:0, one launch (start us, length us, event | category | flops | bytes accessed | tf_op | source)
XLA Modules:
  0.0 50.6 jit_solution(16261040189180100906)
XLA Ops:
  0.6 48.3 %analyse.1 = (f32[4,80,2304]{2,1,0:T(8,128)S(1)}, f32[2,256]{1,0:T(2,128)S(1)}) custom-call(s32[2,256]{1,0:T(2,128)} %cell_hbm.1, f32[2,256]{1,0:T(2,128)} %frac_hbm.1, f32[2,256]{1,0:T(2,128)} %value_hbm.1, f32[2,256]{1,0:T(2,128)} %var_hbm.1, f32[2,4,256]{2,1,0:T(4,128)} %bitcast.1, f32[80,4,2304]{2,1,0:T(4,128)} %ens_hbm.1, bf16[2,64,2304]{2,1,0:T(8,128)(2,1)} %loc_hbm.1), custom_call_target="tpu_custom_call" | custom-call | tf_op jit(solution)/shard_map/analyse/pallas_call | solution.py:359
  48.9 1.6 %hand_over.1 = (f32[80,4,2304]{2,1,0:T(4,128)}, f32[2,256]{1,0:T(2,128)}) custom-call(f32[4,80,2304]{2,1,0:T(8,128)S(1)} %get-tuple-element.4.state, f32[2,256]{1,0:T(2,128)S(1)} %get-tuple-element.5.means), custom_call_target="tpu_custom_call" | custom-call | tf_op jit(solution)/shard_map/hand_over/pallas_call | solution.py:415

commit v4 on v3

--- a/solution.py
+++ b/solution.py
@@ -14,7 +14,7 @@
 BF16 = jnp.bfloat16
 SKEW = 3
 STEPS_FIRST = (3, 3, 2)
-STEPS_LATER = (4, 3, 2)
+STEPS_LATER = (3, 3, 2)
 
 
 def kernel(
@@ -245,8 +245,8 @@
         for level in range(lev_rows):
             lev_s[level] = jnp.broadcast_to(lev_ref[b, level : level + 1, :], (LANES, n_obs)).T
 
-    def update(b, c):
-        at = pl.ds(pl.multiple_of(c * width, width), width)
+    def update(b, c, span=1):
+        at = pl.ds(pl.multiple_of(c * width, width), span * width)
         dev = dev_s[:, :members]
         gain = gain_s[...]
         loc = gat[b, :, at].astype(F32)
@@ -254,7 +254,7 @@
         now = [state[level, :, at] for level in levels]
         centred = [(x - jnp.sum(x, axis=0, keepdims=True) / members).astype(BF16) for x in now]
         cross = [jnp.dot(dev, x, preferred_element_type=F32) for x in centred]
-        height = [jnp.concatenate([lev_s[level]] * wide, axis=1) for level in levels]
+        height = [jnp.concatenate([lev_s[level]] * (span * wide), axis=1) for level in levels]
         mixed = [((height[level] * loc) * cross[level]).astype(BF16) for level in levels]
         new = [now[level] + jnp.dot(gain, mixed[level], preferred_element_type=F32) for level in levels]
         for level in levels:
@@ -289,8 +289,7 @@
 
         def double(s, carry):
             forward(b, s)
-            update(b, 2 * (s - done))
-            update(b, 2 * (s - done) + 1)
+            update(b, 2 * (s - done), 2)
             return carry
 
         def single(s, carry):

time: 50.7 us -> 50.7 us (level)
  no operation moved by 1% of the time
where the time goes in v4:
time: 50.7 us; the launch traced here: 50.5 us
  Pallas kernels  49.9 us (98%)
  between operations  0.64 us (1%)
    pallas_call x1, Pallas kernels, analyse(): pl.pallas_call(functools.partial(kernel, n_slab, n_lev), out_shape=[pltpu...  48.2 us
    pallas_call x1, Pallas kernels, hand_over(): pl.pallas_call(hand_over_kernel, out_shape=[pltpu.HBM((members, lev_rows,...  1.64 us

profile of v4, /device:TPU:0, one launch (start us, length us, event | category | flops | bytes accessed | tf_op | source)
XLA Modules:
  0.0 50.5 jit_solution(14688990611350123407)
XLA Ops:
  0.6 48.2 %analyse.1 = (f32[4,80,2304]{2,1,0:T(8,128)S(1)}, f32[2,256]{1,0:T(2,128)S(1)}) custom-call(s32[2,256]{1,0:T(2,128)} %cell_hbm.1, f32[2,256]{1,0:T(2,128)} %frac_hbm.1, f32[2,256]{1,0:T(2,128)} %value_hbm.1, f32[2,256]{1,0:T(2,128)} %var_hbm.1, f32[2,4,256]{2,1,0:T(4,128)} %bitcast.1, f32[80,4,2304]{2,1,0:T(4,128)} %ens_hbm.1, bf16[2,64,2304]{2,1,0:T(8,128)(2,1)} %loc_hbm.1), custom_call_target="tpu_custom_call" | custom-call | tf_op jit(solution)/shard_map/analyse/pallas_call | solution.py:358
  48.9 1.6 %hand_over.1 = (f32[80,4,2304]{2,1,0:T(4,128)}, f32[2,256]{1,0:T(2,128)}) custom-call(f32[4,80,2304]{2,1,0:T(8,128)S(1)} %get-tuple-element.4.state, f32[2,256]{1,0:T(2,128)S(1)} %get-tuple-element.5.means), custom_call_target="tpu_custom_call" | custom-call | tf_op jit(solution)/shard_map/hand_over/pallas_call | solution.py:414
